TPU v7x, 32 devices: a whole 2x2x4 slice. The times are simulated.
32 devices in a mesh: expert: 16 (over z, y, core), tensor: 2 (over x).
Axes of the slice: x: 2, y: 2, z: 4, core: 2. Of those that a mesh axis runs over, the one named last changes fastest.
Arguments:
- tokens: bfloat16 [64, 256, 1280], P(('expert', 'tensor')), may hold values from -6 to 6
- slot_keys: bfloat16 [1280, 16], replicated, may hold values from -6 to 6
- logit_scale: float32 [], replicated, may hold values from 40 to 80
- w_in: bfloat16 [16, 1280, 3584], P('expert', None, 'tensor'), may hold values from -0.625 to 0.625
- b_in: bfloat16 [16, 3584], P('expert', 'tensor'), may hold values from -3 to 3
- w_out: bfloat16 [16, 3584, 1280], P('expert', 'tensor'), may hold values from -0.09375 to 0.09375
- b_out: bfloat16 [16, 1280], P('expert'), may hold values from -3 to 3
Outputs:
- mixed: bfloat16 [64, 256, 1280], P(('expert', 'tensor'))
All inputs are finite; a program needn't handle non-finite values.
Results may differ from a plain program's by a relative error of at most 0.0071.
Values may be sent and summed in bfloat16 or wider, within the bound.
A program may use at most 64 MiB of HBM per device.

v0:
```python
import functools

import jax
import jax.numpy as jnp
from jax import lax
from jax.experimental import pallas as pl
from jax.experimental.pallas import tpu as pltpu
from jax.sharding import PartitionSpec as P

EPS = 1e-06
MESH = pl.DeviceIdType.MESH
NT = (((1,), (1,)), ((), ()))


def kernel(
    experts, tensors, cuts,
    tokens_hbm, keys_ref, scale_ref, w_in_hbm, b_in_ref, w_out_hbm, b_out_ref,
    out_ref,
    tok, w_in, w_out, send1, recv1, x2, hidden, comb, *rest,
):
    n_cut = len(cuts)
    send2, recv2 = rest[:n_cut], rest[n_cut:2 * n_cut]
    load_sem, send_sem1, recv_sem1, send_sem2, recv_sem2 = rest[2 * n_cut:]
    images, seq, width = tok.shape
    slots = keys_ref.shape[0]
    rows = slots * images
    devices = experts * tensors
    e, t = lax.axis_index("expert"), lax.axis_index("tensor")
    me = e * tensors + t
    home = t * experts + e

    loads = [
        pltpu.make_async_copy(tokens_hbm, tok, load_sem.at[0]),
        pltpu.make_async_copy(w_in_hbm.at[0], w_in, load_sem.at[1]),
        pltpu.make_async_copy(w_out_hbm.at[0], w_out, load_sem.at[2]),
    ]
    for load in loads:
        load.start()

    def peer(step):
        j = lax.rem(me + step, devices)
        je, jt = j // tensors, lax.rem(j, tensors)
        return j, je, {"expert": je, "tensor": jt}

    barrier = pltpu.get_barrier_semaphore()

    @pl.loop(1, devices)
    def _(step):
        pl.semaphore_signal(barrier, inc=1, device_id=peer(step)[2], device_id_type=MESH)

    row_slot = lax.broadcasted_iota(jnp.int32, (rows, slots), 0) // images
    col_slot = lax.broadcasted_iota(jnp.int32, (rows, slots), 1)
    spread = jnp.where(row_slot == col_slot, 1.0, 0.0).astype(jnp.bfloat16)
    keys_t = jnp.dot(spread, keys_ref[...], preferred_element_type=jnp.float32)
    key_inv = lax.rsqrt(jnp.sum(keys_t * keys_t, axis=1, keepdims=True) + EPS)
    key_gain = key_inv * scale_ref[0]
    keys_b = keys_t.astype(jnp.bfloat16)

    loads[0].wait()
    flat = tok[...].reshape(images * seq, width)
    raw = lax.dot_general(keys_b, flat, NT, preferred_element_type=jnp.float32)
    part = jnp.zeros((images * seq, 128), jnp.float32)
    for c in range(width // 128):
        piece = flat[:, c * 128:(c + 1) * 128].astype(jnp.float32)
        part = part + piece * piece
    row_sq = lax.dot_general(
        jnp.ones((8, 128), jnp.float32), part, NT,
        precision=lax.Precision.HIGHEST, preferred_element_type=jnp.float32,
    )[0:1]
    logits = key_gain * lax.rsqrt(row_sq + EPS) * raw
    row_image = lax.broadcasted_iota(jnp.int32, logits.shape, 0) % images
    col_image = lax.broadcasted_iota(jnp.int32, logits.shape, 1) // seq
    expo = jnp.where(row_image == col_image, jnp.exp(logits), 0.0)
    dispatch = (expo / jnp.sum(expo, axis=1, keepdims=True)).astype(jnp.bfloat16)
    slot_in = jnp.dot(dispatch, flat, preferred_element_type=jnp.float32).astype(jnp.bfloat16)
    for s in range(slots):
        send1[s] = slot_in[s * images:(s + 1) * images]

    pl.semaphore_wait(barrier, devices - 1)

    own = pltpu.make_async_copy(send1.at[e], recv1.at[me], recv_sem1)
    own.start()

    @pl.loop(1, devices)
    def _(step):
        _, je, device = peer(step)
        pltpu.make_async_remote_copy(
            src_ref=send1.at[je], dst_ref=recv1.at[me], send_sem=send_sem1, recv_sem=recv_sem1,
            device_id=device, device_id_type=MESH,
        ).start()

    combine = expo / jnp.sum(expo, axis=0, keepdims=True)
    comb[...] = jnp.concatenate([combine] * tensors, axis=0).T.astype(jnp.bfloat16)

    loads[1].wait()
    pltpu.make_async_copy(recv1, recv1, recv_sem1).wait()
    x = recv1[...].reshape(devices * images, width)
    half = w_in.shape[1]
    for c in range(0, half, 256):
        size = min(256, half - c)
        pre = jnp.dot(x, w_in[:, c:c + size], preferred_element_type=jnp.float32)
        pre = pre + b_in_ref[:, c:c + size].astype(jnp.float32)
        hidden[:, c:c + size] = jax.nn.gelu(pre).astype(jnp.bfloat16)

    loads[2].wait()
    h = hidden[...]
    first_half = jnp.where(t == 0, 1.0, 0.0)
    for c, (start, size) in enumerate(cuts):
        y = jnp.dot(h, w_out[:, start:start + size], preferred_element_type=jnp.float32)
        y = y + b_out_ref[:, start:start + size].astype(jnp.float32) * first_half
        y = y.astype(jnp.bfloat16)
        send2[c][...] = y.reshape(devices, images, size)
        pltpu.make_async_copy(send2[c].at[me], recv2[c].at[home], recv_sem2.at[c]).start()

        @pl.loop(1, devices)
        def _(step):
            j, _, device = peer(step)
            pltpu.make_async_remote_copy(
                src_ref=send2[c].at[j], dst_ref=recv2[c].at[home],
                send_sem=send_sem2.at[c], recv_sem=recv_sem2.at[c],
                device_id=device, device_id_type=MESH,
            ).start()

    cm = comb[...]
    for c, (start, size) in enumerate(cuts):
        pltpu.make_async_copy(recv2[c], recv2[c], recv_sem2.at[c]).wait()
        mixed = jnp.dot(cm, recv2[c][...].reshape(devices * images, size), preferred_element_type=jnp.float32)
        out_ref[:, :, start:start + size] = mixed.astype(jnp.bfloat16).reshape(images, seq, size)

    first = recv1.at[pl.ds(0, devices - 1)]
    pltpu.make_async_copy(first, first, send_sem1).wait()
    for c in range(n_cut):
        block = recv2[c].at[pl.ds(0, devices - 1)]
        pltpu.make_async_copy(block, block, send_sem2.at[c]).wait()


def local(experts, tensors, tokens, slot_keys, logit_scale, w_in, b_in, w_out, b_out):
    images, seq, width = tokens.shape
    slots = slot_keys.shape[1]
    half = w_in.shape[2]
    devices = experts * tensors
    cuts = [(0, width)]
    bf16 = jnp.bfloat16
    return pl.pallas_call(
        functools.partial(kernel, experts, tensors, cuts),
        out_shape=pltpu.VMEM(tokens.shape, bf16),
        in_specs=[
            pl.BlockSpec(memory_space=pltpu.HBM),
            pl.BlockSpec(memory_space=pltpu.VMEM),
            pl.BlockSpec(memory_space=pltpu.SMEM),
            pl.BlockSpec(memory_space=pltpu.HBM),
            pl.BlockSpec(memory_space=pltpu.VMEM),
            pl.BlockSpec(memory_space=pltpu.HBM),
            pl.BlockSpec(memory_space=pltpu.VMEM),
        ],
        out_specs=pl.BlockSpec(memory_space=pltpu.VMEM),
        scratch_shapes=[
            pltpu.VMEM((images, seq, width), bf16),
            pltpu.VMEM((width, half), bf16),
            pltpu.VMEM((half, width), bf16),
            pltpu.VMEM((slots, images, width), bf16),
            pltpu.VMEM((devices, images, width), bf16),
            pltpu.VMEM((devices * images, width), bf16),
            pltpu.VMEM((devices * images, half), bf16),
            pltpu.VMEM((images * seq, tensors * slots * images), bf16),
            *[pltpu.VMEM((devices, images, size), bf16) for _, size in cuts],
            *[pltpu.VMEM((devices, images, size), bf16) for _, size in cuts],
            pltpu.SemaphoreType.DMA((3,)),
            pltpu.SemaphoreType.DMA,
            pltpu.SemaphoreType.DMA,
            pltpu.SemaphoreType.DMA((len(cuts),)),
            pltpu.SemaphoreType.DMA((len(cuts),)),
        ],
        compiler_params=pltpu.CompilerParams(collective_id=0, has_side_effects=True, vmem_limit_bytes=61 * 2**20),
    )(tokens, slot_keys.T, logit_scale.reshape(1), w_in, b_in, w_out, b_out)


def solution(mesh):
    placed = (
        P(("expert", "tensor"), None, None),
        P(),
        P(),
        P("expert", None, "tensor"),
        P("expert", "tensor"),
        P("expert", "tensor", None),
        P("expert", None),
    )
    return jax.shard_map(
        functools.partial(local, mesh.shape["expert"], mesh.shape["tensor"]),
        mesh=mesh,
        in_specs=placed,
        out_specs=P(("expert", "tensor"), None, None),
        check_vma=False,
    )
```

profile of v0, /device:TPU:0, one launch (start us, length us, event | category | flops | bytes accessed | tf_op | source)
XLA Modules:
  0.0 23.0 jit_solution(7527595345838734450)
XLA Ops:
  0.7 21.3 %shard_map.73 = bf16[2,256,1280]{2,1,0:T(8,128)(2,1)S(1)} custom-call(bf16[2,256,1280]{2,1,0:T(8,128)(2,1)} %tokens_hbm.1, bf16[16,1280]{1,0:T(8,128)(2,1)} %bitcast.3, f32[1]{0:T(128)} %bitcast.2.scale_ref, bf16[1,1280,1792]{2,1,0:T(8,128)(2,1)} %w_in_hbm.1, bf16[1,1792]{1,0:T(2,128)(2,1)} %b_in_ref.1, bf16[1,1792,1280]{2,1,0:T(8,128)(2,1)} %w_out_hbm.1, ...), custom_call_target="tpu_custom_call" | custom-call | tf_op jit(solution)/shard_map/pallas_call | solution.py:144
  22.0 1.1 %copy.9 = bf16[2,256,1280]{2,1,0:T(8,128)(2,1)} copy(bf16[2,256,1280]{2,1,0:T(8,128)(2,1)S(1)} %shard_map.73) | data formatting | bytes 2621440
where the time goes:
time: 23.2 us; the launch traced here: 23 us
  Pallas kernels  21.3 us (92%)
  local copies, waits for them, and re-layouts  1.06 us (5%)
  between operations  0.66 us (3%)
    pallas_call x1, Pallas kernels, local(): pl.pallas_call(functools.partial(kernel, experts, tensors, cuts), out_sha...  21.3 us
    unnamed x1, local copies, waits for them, and re-layouts  1.06 us

commit v1 on v0

v1 whole, which is shorter than its diff:
```python
import functools

import jax
import jax.numpy as jnp
from jax import lax
from jax.experimental import pallas as pl
from jax.experimental.pallas import tpu as pltpu
from jax.sharding import PartitionSpec as P

EPS = 1e-06
LOGICAL = pl.DeviceIdType.LOGICAL
NT = (((1,), (1,)), ((), ()))
UNROLL = 64
TILE = 256
SPLIT = 2


def peers_of(mesh):
    flat = list(mesh.devices.flat)
    devices = len(flat)

    def hops(k):
        a, b = (getattr(d, "coords", (0, 0, 0)) for d in (flat[0], flat[k]))
        return sum(abs(p - q) for p, q in zip(a, b))

    return sorted(range(1, devices), key=lambda k: (-hops(k), -k))


def kernel(
    experts, tensors, steps,
    tokens_hbm, keys_hbm, scale_hbm, w_in_hbm, b_in_hbm, w_out_hbm, b_out_hbm,
    recv2, comb,
    tok, keys_ref, scale_ref, b_in_ref, b_out_ref, w_in, w_out, send1, recv1, hidden, send2,
    load_sem, send_sem1, recv_sem1, send_sem2, recv_sem2,
):
    images, seq, width = tok.shape
    slots = keys_ref.shape[0]
    rows = slots * images
    devices = experts * tensors
    e, t = lax.axis_index("expert"), lax.axis_index("tensor")
    me = e * tensors + t
    home = t * experts + e
    pow2 = devices & (devices - 1) == 0

    def each_peer(body):
        if pow2 and devices <= UNROLL:
            for k in steps:
                body(me ^ k)
        else:
            @pl.loop(1, devices)
            def _(step):
                body(lax.rem(me + step, devices))

    barrier = pltpu.get_barrier_semaphore()
    each_peer(lambda j: pl.semaphore_signal(barrier, inc=1, device_id=j, device_id_type=LOGICAL))

    pairs = [
        (keys_hbm, keys_ref), (scale_hbm, scale_ref), (tokens_hbm, tok), (b_in_hbm, b_in_ref),
        (w_in_hbm.at[0], w_in), (b_out_hbm, b_out_ref), (w_out_hbm.at[0], w_out),
    ]
    loads = [pltpu.make_async_copy(src, dst, load_sem.at[i]) for i, (src, dst) in enumerate(pairs)]
    for load in loads:
        load.start()

    loads[0].wait()
    loads[1].wait()
    row_slot = lax.broadcasted_iota(jnp.int32, (rows, slots), 0) // images
    col_slot = lax.broadcasted_iota(jnp.int32, (rows, slots), 1)
    spread = jnp.where(row_slot == col_slot, 1.0, 0.0).astype(jnp.bfloat16)
    keys_t = jnp.dot(spread, keys_ref[...], preferred_element_type=jnp.float32)
    key_inv = lax.rsqrt(jnp.sum(keys_t * keys_t, axis=1, keepdims=True) + EPS)
    key_gain = key_inv * scale_ref[0]
    keys_b = keys_t.astype(jnp.bfloat16)

    loads[2].wait()
    flat = tok[...].reshape(images * seq, width)
    raw = lax.dot_general(keys_b, flat, NT, preferred_element_type=jnp.float32)
    part = jnp.zeros((images * seq, 128), jnp.float32)
    for c in range(width // 128):
        piece = flat[:, c * 128:(c + 1) * 128].astype(jnp.float32)
        part = part + piece * piece
    row_sq = lax.dot_general(
        jnp.ones((8, 128), jnp.float32), part, NT,
        precision=lax.Precision.HIGHEST, preferred_element_type=jnp.float32,
    )[0:1]
    logits = key_gain * lax.rsqrt(row_sq + EPS) * raw
    row_image = lax.broadcasted_iota(jnp.int32, logits.shape, 0) % images
    col_image = lax.broadcasted_iota(jnp.int32, logits.shape, 1) // seq
    expo = jnp.where(row_image == col_image, jnp.exp(logits), 0.0)
    dispatch = (expo / jnp.sum(expo, axis=1, keepdims=True)).astype(jnp.bfloat16)
    slot_in = jnp.dot(dispatch, flat, preferred_element_type=jnp.float32).astype(jnp.bfloat16)
    for s in range(slots):
        send1[s] = slot_in[s * images:(s + 1) * images]
    recv1[me] = send1[e]
    combine = expo / jnp.sum(expo, axis=0, keepdims=True)
    comb[...] = jnp.concatenate([combine] * tensors, axis=0).T.astype(jnp.bfloat16)

    pl.semaphore_wait(barrier, devices - 1)
    each_peer(lambda j: pltpu.make_async_remote_copy(
        src_ref=send1.at[j // tensors], dst_ref=recv1.at[me], send_sem=send_sem1, recv_sem=recv_sem1,
        device_id=j, device_id_type=LOGICAL,
    ).start())

    for load in loads[3:]:
        load.wait()
    others = recv1.at[pl.ds(0, devices - 1)]
    pltpu.make_async_copy(others, others, recv_sem1).wait()
    x = recv1[...].reshape(devices * images, width)
    half = w_in.shape[1]
    first_half = jnp.where(t == 0, 1.0, 0.0)
    for c in range(0, half, TILE):
        size = min(TILE, half - c)
        pre = jnp.dot(x, w_in[:, c:c + size], preferred_element_type=jnp.float32)
        pre = pre + b_in_ref[:, c:c + size].astype(jnp.float32)
        hidden[:, c:c + size] = jax.nn.gelu(pre).astype(jnp.bfloat16)
    y = jnp.dot(hidden[...], w_out[...], preferred_element_type=jnp.float32)
    y = y + b_out_ref[...].astype(jnp.float32) * first_half
    send2[...] = y.astype(jnp.bfloat16).reshape(devices, images, width)
    recv2[home] = send2[me]
    each_peer(lambda j: pltpu.make_async_remote_copy(
        src_ref=send2.at[j], dst_ref=recv2.at[home], send_sem=send_sem2, recv_sem=recv_sem2,
        device_id=j, device_id_type=LOGICAL,
    ).start())

    pltpu.make_async_copy(others, others, send_sem1).wait()
    block = recv2.at[pl.ds(0, devices - 1)]
    pltpu.make_async_copy(block, block, send_sem2).wait()
    pltpu.make_async_copy(block, block, recv_sem2).wait()


def mix(chunk, recv2, comb, out_hbm, out, sem):
    images, seq, width = out_hbm.shape
    r = recv2[...].reshape(-1, width)
    copies = []
    for c in range(images * seq // chunk):
        mixed = jnp.dot(comb[c * chunk:(c + 1) * chunk], r, preferred_element_type=jnp.float32)
        at = (c * chunk // seq, pl.ds(c * chunk % seq, chunk))
        out[at[0], at[1]] = mixed.astype(jnp.bfloat16)
        copies.append(pltpu.make_async_copy(out.at[at[0], at[1]], out_hbm.at[at[0], at[1]], sem.at[c]))
        copies[-1].start()
    for copy in copies:
        copy.wait()


def local(experts, tensors, steps, tokens, slot_keys, logit_scale, w_in, b_in, w_out, b_out):
    images, seq, width = tokens.shape
    slots = slot_keys.shape[1]
    half = w_in.shape[2]
    devices = experts * tensors
    bf16 = jnp.bfloat16
    recv2, comb = pl.pallas_call(
        functools.partial(kernel, experts, tensors, steps),
        out_shape=[
            pltpu.VMEM((devices, images, width), bf16),
            pltpu.VMEM((images * seq, tensors * slots * images), bf16),
        ],
        in_specs=[pl.BlockSpec(memory_space=pltpu.HBM)] * 7,
        out_specs=[pl.BlockSpec(memory_space=pltpu.VMEM)] * 2,
        scratch_shapes=[
            pltpu.VMEM((images, seq, width), bf16),
            pltpu.VMEM((slots, width), bf16),
            pltpu.SMEM((1,), jnp.float32),
            pltpu.VMEM((1, half), bf16),
            pltpu.VMEM((1, width), bf16),
            pltpu.VMEM((width, half), bf16),
            pltpu.VMEM((half, width), bf16),
            pltpu.VMEM((slots, images, width), bf16),
            pltpu.VMEM((devices, images, width), bf16),
            pltpu.VMEM((devices * images, half), bf16),
            pltpu.VMEM((devices, images, width), bf16),
            pltpu.SemaphoreType.DMA((7,)),
            pltpu.SemaphoreType.DMA,
            pltpu.SemaphoreType.DMA,
            pltpu.SemaphoreType.DMA,
            pltpu.SemaphoreType.DMA,
        ],
        compiler_params=pltpu.CompilerParams(collective_id=0, has_side_effects=True, vmem_limit_bytes=55 * 2**20),
    )(tokens, slot_keys.T, logit_scale.reshape(1), w_in, b_in, w_out, b_out)
    chunk = seq // SPLIT
    return pl.pallas_call(
        functools.partial(mix, chunk),
        out_shape=jax.ShapeDtypeStruct(tokens.shape, bf16),
        in_specs=[pl.BlockSpec(memory_space=pltpu.VMEM)] * 2,
        out_specs=pl.BlockSpec(memory_space=pltpu.HBM),
        scratch_shapes=[
            pltpu.VMEM(tokens.shape, bf16),
            pltpu.SemaphoreType.DMA((images * seq // chunk,)),
        ],
        compiler_params=pltpu.CompilerParams(vmem_limit_bytes=16 * 2**20),
    )(recv2, comb)


def solution(mesh):
    placed = (
        P(("expert", "tensor"), None, None),
        P(),
        P(),
        P("expert", None, "tensor"),
        P("expert", "tensor"),
        P("expert", "tensor", None),
        P("expert", None),
    )
    return jax.shard_map(
        functools.partial(local, mesh.shape["expert"], mesh.shape["tensor"], peers_of(mesh)),
        mesh=mesh,
        in_specs=placed,
        out_specs=P(("expert", "tensor"), None, None),
        check_vma=False,
    )
```

time: 23.2 us -> 21.7 us (0.935)
  local copies, waits for them, and re-layouts: 1.06 us -> 0 us
  Pallas kernels: 21.3 us -> 20.9 us
    unnamed x1 -> x0, local copies, waits for them, and re-layouts: 1.06 us -> none
    pallas_call x1 -> x2, Pallas kernels: 21.3 us -> 20.9 us  [the longest x1 19.5 us: local(): pl.pallas_call(functools.partial(kernel, experts, tensors, steps), out_sh...]
where the time goes in v1:
time: 21.7 us; the launch traced here: 21.5 us
  Pallas kernels  20.9 us (96%)
  between operations  0.66 us (3%)
    pallas_call x1, Pallas kernels, local(): pl.pallas_call(functools.partial(kernel, experts, tensors, steps), out_sh...  19.5 us
    pallas_call x1, Pallas kernels, local(): pl.pallas_call(functools.partial(mix, chunk), out_shape=jax.ShapeDtypeStr...  1.33 us

profile of v1, /device:TPU:0, one launch (start us, length us, event | category | flops | bytes accessed | tf_op | source)
XLA Modules:
  0.0 21.5 jit_solution(3938899268780464193)
XLA Ops:
  0.7 19.5 %shard_map.73 = (bf16[32,2,1280]{2,1,0:T(2,128)(2,1)S(1)}, bf16[512,64]{1,0:T(8,128)(2,1)S(1)}) custom-call(bf16[2,256,1280]{2,1,0:T(8,128)(2,1)} %tokens_hbm.1, bf16[16,1280]{1,0:T(8,128)(2,1)} %bitcast.3, f32[1]{0:T(128)} %bitcast.2.scale_hbm, bf16[1,1280,1792]{2,1,0:T(8,128)(2,1)} %w_in_hbm.1, bf16[1,1792]{1,0:T(2,128)(2,1)} %b_in_hbm.1, ...), custom_call_target="tpu_custom_call" | custom-call | tf_op jit(solution)/shard_map/pallas_call | solution.py:151
  20.2 1.3 %shard_map.74 = bf16[2,256,1280]{2,1,0:T(8,128)(2,1)} custom-call(bf16[32,2,1280]{2,1,0:T(2,128)(2,1)S(1)} %get-tuple-element.7.recv2, bf16[512,64]{1,0:T(8,128)(2,1)S(1)} %get-tuple-element.8.comb), custom_call_target="tpu_custom_call" | custom-call | tf_op jit(solution)/shard_map/pallas_call | solution.py:180

commit v2 on v1

--- a/solution.py
+++ b/solution.py
@@ -17,17 +17,23 @@
 
 def peers_of(mesh):
     flat = list(mesh.devices.flat)
-    devices = len(flat)
-
-    def hops(k):
-        a, b = (getattr(d, "coords", (0, 0, 0)) for d in (flat[0], flat[k]))
-        return sum(abs(p - q) for p, q in zip(a, b))
-
-    return sorted(range(1, devices), key=lambda k: (-hops(k), -k))
+    where = [tuple(getattr(d, "coords", None) or (0, 0, 0)) for d in flat]
+    away = [[abs(p - q) for p, q in zip(w, where[0])] for w in where]
+    axis = max(range(len(where[0])), key=lambda a: max(w[a] for w in away))
+    groups = {}
+    for k in sorted(range(1, len(flat)), key=lambda k: (-sum(away[k]), -k)):
+        groups.setdefault(away[k][axis], []).append(k)
+    steps = []
+    while any(groups.values()):
+        for g in sorted(groups, reverse=True):
+            steps += groups[g][:1]
+            del groups[g][:1]
+    first = [k for k in range(len(flat)) if where[k] == where[0]][:2]
+    return steps, first
 
 
 def kernel(
-    experts, tensors, steps,
+    experts, tensors, order,
     tokens_hbm, keys_hbm, scale_hbm, w_in_hbm, b_in_hbm, w_out_hbm, b_out_hbm,
     recv2, comb,
     tok, keys_ref, scale_ref, b_in_ref, b_out_ref, w_in, w_out, send1, recv1, hidden, send2,
@@ -40,12 +46,20 @@
     e, t = lax.axis_index("expert"), lax.axis_index("tensor")
     me = e * tensors + t
     home = t * experts + e
+    steps, first = order
     pow2 = devices & (devices - 1) == 0
 
-    def each_peer(body):
+    def each_peer(body, ahead=()):
         if pow2 and devices <= UNROLL:
+            for j in ahead:
+                pl.when(me != j)(functools.partial(body, j))
             for k in steps:
-                body(me ^ k)
+                j = me ^ k
+                if ahead:
+                    rest = functools.reduce(jnp.logical_and, [j != a for a in ahead])
+                    pl.when(rest)(functools.partial(body, j))
+                else:
+                    body(j)
         else:
             @pl.loop(1, devices)
             def _(step):
@@ -120,7 +134,7 @@
     each_peer(lambda j: pltpu.make_async_remote_copy(
         src_ref=send2.at[j], dst_ref=recv2.at[home], send_sem=send_sem2, recv_sem=recv_sem2,
         device_id=j, device_id_type=LOGICAL,
-    ).start())
+    ).start(), first)
 
     pltpu.make_async_copy(others, others, send_sem1).wait()
     block = recv2.at[pl.ds(0, devices - 1)]
@@ -142,14 +156,14 @@
         copy.wait()
 
 
-def local(experts, tensors, steps, tokens, slot_keys, logit_scale, w_in, b_in, w_out, b_out):
+def local(experts, tensors, order, tokens, slot_keys, logit_scale, w_in, b_in, w_out, b_out):
     images, seq, width = tokens.shape
     slots = slot_keys.shape[1]
     half = w_in.shape[2]
     devices = experts * tensors
     bf16 = jnp.bfloat16
     recv2, comb = pl.pallas_call(
-        functools.partial(kernel, experts, tensors, steps),
+        functools.partial(kernel, experts, tensors, order),
         out_shape=[
             pltpu.VMEM((devices, images, width), bf16),
             pltpu.VMEM((images * seq, tensors * slots * images), bf16),

time: 21.7 us -> 20.7 us (0.954)
  Pallas kernels: 20.9 us -> 19.9 us
    pallas_call x1, Pallas kernels: 19.5 us -> 18.5 us  [local(): pl.pallas_call(functools.partial(kernel, experts, tensors, order), out_sh...]
where the time goes in v2:
time: 20.7 us; the launch traced here: 20.5 us
  Pallas kernels  19.9 us (96%)
  between operations  0.66 us (3%)
    pallas_call x1, Pallas kernels, local(): pl.pallas_call(functools.partial(kernel, experts, tensors, order), out_sh...  18.5 us
    pallas_call x1, Pallas kernels, local(): pl.pallas_call(functools.partial(mix, chunk), out_shape=jax.ShapeDtypeStr...  1.33 us

profile of v2, /device:TPU:0, one launch (start us, length us, event | category | flops | bytes accessed | tf_op | source)
XLA Modules:
  0.0 20.5 jit_solution(4286716931652706623)
XLA Ops:
  0.7 18.5 %shard_map.73 = (bf16[32,2,1280]{2,1,0:T(2,128)(2,1)S(1)}, bf16[512,64]{1,0:T(8,128)(2,1)S(1)}) custom-call(bf16[2,256,1280]{2,1,0:T(8,128)(2,1)} %tokens_hbm.1, bf16[16,1280]{1,0:T(8,128)(2,1)} %bitcast.3, f32[1]{0:T(128)} %bitcast.2.scale_hbm, bf16[1,1280,1792]{2,1,0:T(8,128)(2,1)} %w_in_hbm.1, bf16[1,1792]{1,0:T(2,128)(2,1)} %b_in_hbm.1, ...), custom_call_target="tpu_custom_call" | custom-call | tf_op jit(solution)/shard_map/pallas_call | solution.py:165
  19.2 1.3 %shard_map.74 = bf16[2,256,1280]{2,1,0:T(8,128)(2,1)} custom-call(bf16[32,2,1280]{2,1,0:T(2,128)(2,1)S(1)} %get-tuple-element.7.recv2, bf16[512,64]{1,0:T(8,128)(2,1)S(1)} %get-tuple-element.8.comb), custom_call_target="tpu_custom_call" | custom-call | tf_op jit(solution)/shard_map/pallas_call | solution.py:194

commit v3 on v2

--- a/solution.py
+++ b/solution.py
@@ -11,7 +11,7 @@
 LOGICAL = pl.DeviceIdType.LOGICAL
 NT = (((1,), (1,)), ((), ()))
 UNROLL = 64
-TILE = 256
+TILE = 128
 SPLIT = 2
 
 
@@ -127,9 +127,12 @@
         pre = jnp.dot(x, w_in[:, c:c + size], preferred_element_type=jnp.float32)
         pre = pre + b_in_ref[:, c:c + size].astype(jnp.float32)
         hidden[:, c:c + size] = jax.nn.gelu(pre).astype(jnp.bfloat16)
-    y = jnp.dot(hidden[...], w_out[...], preferred_element_type=jnp.float32)
-    y = y + b_out_ref[...].astype(jnp.float32) * first_half
-    send2[...] = y.astype(jnp.bfloat16).reshape(devices, images, width)
+    h = hidden[...]
+    part = width // 2 if width % 256 == 0 else width
+    for c in range(0, width, part):
+        y = jnp.dot(h, w_out[:, c:c + part], preferred_element_type=jnp.float32)
+        y = y + b_out_ref[:, c:c + part].astype(jnp.float32) * first_half
+        send2[:, :, c:c + part] = y.astype(jnp.bfloat16).reshape(devices, images, part)
     recv2[home] = send2[me]
     each_peer(lambda j: pltpu.make_async_remote_copy(
         src_ref=send2.at[j], dst_ref=recv2.at[home], send_sem=send_sem2, recv_sem=recv_sem2,
@@ -145,15 +148,13 @@
 def mix(chunk, recv2, comb, out_hbm, out, sem):
     images, seq, width = out_hbm.shape
     r = recv2[...].reshape(-1, width)
-    copies = []
-    for c in range(images * seq // chunk):
-        mixed = jnp.dot(comb[c * chunk:(c + 1) * chunk], r, preferred_element_type=jnp.float32)
-        at = (c * chunk // seq, pl.ds(c * chunk % seq, chunk))
-        out[at[0], at[1]] = mixed.astype(jnp.bfloat16)
-        copies.append(pltpu.make_async_copy(out.at[at[0], at[1]], out_hbm.at[at[0], at[1]], sem.at[c]))
-        copies[-1].start()
-    for copy in copies:
-        copy.wait()
+    for c in range(0, images * seq, chunk):
+        at = c // seq, pl.ds(c % seq, chunk)
+        for n in range(0, width, TILE):
+            mixed = jnp.dot(comb[c:c + chunk], r[:, n:n + TILE], preferred_element_type=jnp.float32)
+            out[at[0], at[1], n:n + TILE] = mixed.astype(jnp.bfloat16)
+        pltpu.make_async_copy(out.at[at], out_hbm.at[at], sem).start()
+    pltpu.make_async_copy(out, out_hbm, sem).wait()
 
 
 def local(experts, tensors, order, tokens, slot_keys, logit_scale, w_in, b_in, w_out, b_out):
@@ -198,7 +199,7 @@
         out_specs=pl.BlockSpec(memory_space=pltpu.HBM),
         scratch_shapes=[
             pltpu.VMEM(tokens.shape, bf16),
-            pltpu.SemaphoreType.DMA((images * seq // chunk,)),
+            pltpu.SemaphoreType.DMA,
         ],
         compiler_params=pltpu.CompilerParams(vmem_limit_bytes=16 * 2**20),
     )(recv2, comb)

time: 20.7 us -> 20.4 us (0.986)
  Pallas kernels: 19.9 us -> 19.6 us
    pallas_call x1, Pallas kernels: 18.5 us -> 18.3 us  [local(): pl.pallas_call(functools.partial(kernel, experts, tensors, order), out_sh...]
where the time goes in v3:
time: 20.4 us; the launch traced here: 20.2 us
  Pallas kernels  19.6 us (96%)
  between operations  0.66 us (3%)
    pallas_call x1, Pallas kernels, local(): pl.pallas_call(functools.partial(kernel, experts, tensors, order), out_sh...  18.3 us
    pallas_call x1, Pallas kernels, local(): pl.pallas_call(functools.partial(mix, chunk), out_shape=jax.ShapeDtypeStr...  1.3 us

profile of v3, /device:TPU:0, one launch (start us, length us, event | category | flops | bytes accessed | tf_op | source)
XLA Modules:
  0.0 20.2 jit_solution(9930788719832021233)
XLA Ops:
  0.7 18.3 %shard_map.73 = (bf16[32,2,1280]{2,1,0:T(2,128)(2,1)S(1)}, bf16[512,64]{1,0:T(8,128)(2,1)S(1)}) custom-call(bf16[2,256,1280]{2,1,0:T(8,128)(2,1)} %tokens_hbm.1, bf16[16,1280]{1,0:T(8,128)(2,1)} %bitcast.3, f32[1]{0:T(128)} %bitcast.2.scale_hbm, bf16[1,1280,1792]{2,1,0:T(8,128)(2,1)} %w_in_hbm.1, bf16[1,1792]{1,0:T(2,128)(2,1)} %b_in_hbm.1, ...), custom_call_target="tpu_custom_call" | custom-call | tf_op jit(solution)/shard_map/pallas_call | solution.py:166
  18.9 1.3 %shard_map.74 = bf16[2,256,1280]{2,1,0:T(8,128)(2,1)} custom-call(bf16[32,2,1280]{2,1,0:T(2,128)(2,1)S(1)} %get-tuple-element.7.recv2, bf16[512,64]{1,0:T(8,128)(2,1)S(1)} %get-tuple-element.8.comb), custom_call_target="tpu_custom_call" | custom-call | tf_op jit(solution)/shard_map/pallas_call | solution.py:195

commit v4 on v3

--- a/solution.py
+++ b/solution.py
@@ -29,7 +29,9 @@
             steps += groups[g][:1]
             del groups[g][:1]
     first = [k for k in range(len(flat)) if where[k] == where[0]][:2]
-    return steps, first
+    hops = [sum(a) for a in away]
+    last = sorted((k for k in range(len(flat)) if 0 < hops[k] >= max(hops) - 1), key=lambda k: (-hops[k], -away[k][axis], -k))
+    return steps, first, last
 
 
 def kernel(
@@ -46,7 +48,7 @@
     e, t = lax.axis_index("expert"), lax.axis_index("tensor")
     me = e * tensors + t
     home = t * experts + e
-    steps, first = order
+    steps, first, last = order
     pow2 = devices & (devices - 1) == 0
 
     def each_peer(body, ahead=()):
@@ -113,7 +115,7 @@
     each_peer(lambda j: pltpu.make_async_remote_copy(
         src_ref=send1.at[j // tensors], dst_ref=recv1.at[me], send_sem=send_sem1, recv_sem=recv_sem1,
         device_id=j, device_id_type=LOGICAL,
-    ).start())
+    ).start(), last)
 
     for load in loads[3:]:
         load.wait()

time: 20.4 us -> 20 us (0.980)
  Pallas kernels: 19.6 us -> 19.2 us
    pallas_call x1, Pallas kernels: 18.3 us -> 17.9 us  [local(): pl.pallas_call(functools.partial(kernel, experts, tensors, order), out_sh...]
where the time goes in v4:
time: 20 us; the launch traced here: 19.8 us
  Pallas kernels  19.2 us (96%)
  between operations  0.66 us (3%)
    pallas_call x1, Pallas kernels, local(): pl.pallas_call(functools.partial(kernel, experts, tensors, order), out_sh...  17.9 us
    pallas_call x1, Pallas kernels, local(): pl.pallas_call(functools.partial(mix, chunk), out_shape=jax.ShapeDtypeStr...  1.29 us

profile of v4, /device:TPU:0, one launch (start us, length us, event | category | flops | bytes accessed | tf_op | source)
XLA Modules:
  0.0 19.8 jit_solution(1915687671653425172)
XLA Ops:
  0.7 17.9 %shard_map.73 = (bf16[32,2,1280]{2,1,0:T(2,128)(2,1)S(1)}, bf16[512,64]{1,0:T(8,128)(2,1)S(1)}) custom-call(bf16[2,256,1280]{2,1,0:T(8,128)(2,1)} %tokens_hbm.1, bf16[16,1280]{1,0:T(8,128)(2,1)} %bitcast.3, f32[1]{0:T(128)} %bitcast.2.scale_hbm, bf16[1,1280,1792]{2,1,0:T(8,128)(2,1)} %w_in_hbm.1, bf16[1,1792]{1,0:T(2,128)(2,1)} %b_in_hbm.1, ...), custom_call_target="tpu_custom_call" | custom-call | tf_op jit(solution)/shard_map/pallas_call | solution.py:168
  18.5 1.3 %shard_map.74 = bf16[2,256,1280]{2,1,0:T(8,128)(2,1)} custom-call(bf16[32,2,1280]{2,1,0:T(2,128)(2,1)S(1)} %get-tuple-element.7.recv2, bf16[512,64]{1,0:T(8,128)(2,1)S(1)} %get-tuple-element.8.comb), custom_call_target="tpu_custom_call" | custom-call | tf_op jit(solution)/shard_map/pallas_call | solution.py:197

commit v5 on v4

--- a/solution.py
+++ b/solution.py
@@ -67,16 +67,16 @@
             def _(step):
                 body(lax.rem(me + step, devices))
 
-    barrier = pltpu.get_barrier_semaphore()
-    each_peer(lambda j: pl.semaphore_signal(barrier, inc=1, device_id=j, device_id_type=LOGICAL))
-
     pairs = [
         (keys_hbm, keys_ref), (scale_hbm, scale_ref), (tokens_hbm, tok), (b_in_hbm, b_in_ref),
         (w_in_hbm.at[0], w_in), (b_out_hbm, b_out_ref), (w_out_hbm.at[0], w_out),
     ]
     loads = [pltpu.make_async_copy(src, dst, load_sem.at[i]) for i, (src, dst) in enumerate(pairs)]
-    for load in loads:
+    for load in loads[:3]:
         load.start()
+
+    barrier = pltpu.get_barrier_semaphore()
+    each_peer(lambda j: pl.semaphore_signal(barrier, inc=1, device_id=j, device_id_type=LOGICAL))
 
     loads[0].wait()
     loads[1].wait()
@@ -89,6 +89,8 @@
     keys_b = keys_t.astype(jnp.bfloat16)
 
     loads[2].wait()
+    for load in loads[3:]:
+        load.start()
     flat = tok[...].reshape(images * seq, width)
     raw = lax.dot_general(keys_b, flat, NT, preferred_element_type=jnp.float32)
     part = jnp.zeros((images * seq, 128), jnp.float32)

time: 20 us -> 20 us (level)
  no operation moved by 1% of the time
where the time goes in v5:
time: 20 us; the launch traced here: 19.8 us
  Pallas kernels  19.2 us (96%)
  between operations  0.66 us (3%)
    pallas_call x1, Pallas kernels, local(): pl.pallas_call(functools.partial(kernel, experts, tensors, order), out_sh...  17.9 us
    pallas_call x1, Pallas kernels, local(): pl.pallas_call(functools.partial(mix, chunk), out_shape=jax.ShapeDtypeStr...  1.29 us

profile of v5, /device:TPU:0, one launch (start us, length us, event | category | flops | bytes accessed | tf_op | source)
XLA Modules:
  0.0 19.8 jit_solution(10842101529885098906)
XLA Ops:
  0.7 17.9 %shard_map.73 = (bf16[32,2,1280]{2,1,0:T(2,128)(2,1)S(1)}, bf16[512,64]{1,0:T(8,128)(2,1)S(1)}) custom-call(bf16[2,256,1280]{2,1,0:T(8,128)(2,1)} %tokens_hbm.1, bf16[16,1280]{1,0:T(8,128)(2,1)} %bitcast.3, f32[1]{0:T(128)} %bitcast.2.scale_hbm, bf16[1,1280,1792]{2,1,0:T(8,128)(2,1)} %w_in_hbm.1, bf16[1,1792]{1,0:T(2,128)(2,1)} %b_in_hbm.1, ...), custom_call_target="tpu_custom_call" | custom-call | tf_op jit(solution)/shard_map/pallas_call | solution.py:170
  18.5 1.3 %shard_map.74 = bf16[2,256,1280]{2,1,0:T(8,128)(2,1)} custom-call(bf16[32,2,1280]{2,1,0:T(2,128)(2,1)S(1)} %get-tuple-element.7.recv2, bf16[512,64]{1,0:T(8,128)(2,1)S(1)} %get-tuple-element.8.comb), custom_call_target="tpu_custom_call" | custom-call | tf_op jit(solution)/shard_map/pallas_call | solution.py:199
